TPU v7x, 256 devices: a 4x2x16 block of a 4x16x16 slice. The times are simulated.
256 devices in a mesh: parts: 2 (over y), rows: 128 (over z, x, core).
Axes of the slice: x: 4, y: 2, z: 16, core: 2. Of those that a mesh axis runs over, the one named last changes fastest.
The devices are a block of a 4x16x16 slice.
Arguments:
- latent: bfloat16 [4, 128, 160, 384], P('parts', 'rows'), parts along dimension 0, may hold values from -40 to 40
- conv_cache: bfloat16 [4, 128, 160, 384], P('parts', 'rows'), parts along dimension 0, may hold values from -6 to 6
- time_cache: bfloat16 [4, 128, 160, 384], P('parts', 'rows'), parts along dimension 0, may hold values from -6 to 6
- norm_gain: float32 [384], replicated, may hold values from 0.5 to 2
- norm_shift: float32 [384], replicated, may hold values from -3 to 3
- conv_weight: bfloat16 [3, 3, 3, 384, 384], replicated, may hold values from -0.0625 to 0.0625
- conv_bias: float32 [384], replicated, may hold values from -2 to 2
- time_weight: bfloat16 [3, 384, 768], replicated, may hold values from -0.1875 to 0.1875
- time_bias: float32 [768], replicated, may hold values from -2 to 2
- up_weight: bfloat16 [3, 3, 384, 192], replicated, may hold values from -0.109375 to 0.109375
- up_bias: float32 [192], replicated, may hold values from -2 to 2
Outputs:
- frames_out: bfloat16 [8, 256, 320, 192], P('parts', 'rows'), parts along dimension 0
There are 2 independent parts, one for each index of `parts`. A program takes and returns all parts, laid end to end along the dimension named above; an argument that names none is the same for every part. Nothing has to cross between parts.
All inputs are finite; a program needn't handle non-finite values.
Results may differ from a plain program's by a relative error of at most 0.0056.
Values may be sent and summed in bfloat16 or wider, within the bound.
No kernel may reach another device: no remote copies, remote signals or barrier semaphores. Data moves between devices by JAX's collectives and lax.ppermute only.
A program may use at most 64 MiB of HBM per device.

v0:
```python
import jax
import jax.numpy as jnp
from jax import lax
from jax.sharding import Mesh
from jax.sharding import PartitionSpec as P

GROUPS = 32
ROWS = ("rows_0", "rows_1", "rows_2")
EPSILON = 1e-06


def over_axes(value, axes):
    for axis in axes:
        value = lax.psum(value, axis)
    return value


def with_halo(value, sides, width):
    for axis, dim in sides:
        devices, length = (lax.axis_size(axis), value.shape[dim])
        up = [(i, (i + 1) % devices) for i in range(devices - 1)]
        down = [(j, i) for i, j in up]
        last = lax.slice_in_dim(value, length - width, length, axis=dim)
        initial = lax.slice_in_dim(value, 0, width, axis=dim)
        before = lax.ppermute(last, axis, up)
        after = lax.ppermute(initial, axis, down)
        value = jnp.concatenate([before, value, after], axis=dim)
    return value


def conv_taps(padded, kernel, row_count, col_count):
    channels = padded.shape[-1]
    total = jnp.zeros((padded.shape[0] * row_count * col_count, kernel.shape[-1]), jnp.float32)
    for row_tap in range(3):
        window = jnp.concatenate(
            [
                padded[:, row_tap : row_tap + row_count, col_tap : col_tap + col_count]
                for col_tap in range(3)
            ],
            axis=-1,
        )
        total = total + jnp.dot(
            window.reshape(-1, 3 * channels),
            kernel[row_tap].reshape(3 * channels, -1),
            preferred_element_type=jnp.float32,
        )
    return total


def temporal(block, time_cache, time_weight, time_bias):
    frame_count = block.shape[0]
    channels = block.shape[-1]
    joined = jnp.concatenate([time_cache, block], axis=0)
    window = jnp.concatenate(
        [joined[frame_tap : frame_tap + frame_count] for frame_tap in range(3)], axis=-1
    )
    mixed = (
        jnp.dot(
            window.reshape(-1, 3 * channels),
            time_weight.reshape(3 * channels, -1),
            preferred_element_type=jnp.float32,
        )
        + time_bias
    )
    mixed = mixed.astype(jnp.bfloat16).reshape(block.shape[:-1] + (2, channels))
    return jnp.moveaxis(mixed, 3, 1).reshape((2 * frame_count,) + block.shape[1:])


def on_device(
    latent,
    conv_cache,
    time_cache,
    norm_gain,
    norm_shift,
    conv_weight,
    conv_bias,
    time_weight,
    time_bias,
    up_weight,
    up_bias,
):
    frame_count, row_count, col_count, channels = latent.shape
    signal = latent.astype(jnp.float32)
    grouped = signal.reshape(frame_count, row_count, col_count, GROUPS, channels // GROUPS)
    entries = float(
        frame_count * row_count * lax.axis_size(ROWS) * col_count * (channels // GROUPS)
    )
    total_sum, square_sum = (
        over_axes(jnp.sum(grouped, axis=(0, 1, 2, 4)), ROWS),
        over_axes(jnp.sum(grouped * grouped, axis=(0, 1, 2, 4)), ROWS),
    )
    center = (total_sum / entries).reshape(1, 1, 1, GROUPS, 1)
    spread = square_sum.reshape(1, 1, 1, GROUPS, 1) / entries - center * center
    normed = ((grouped - center) * lax.rsqrt(spread + EPSILON)).reshape(signal.shape)
    active = jax.nn.silu(normed * norm_gain + norm_shift).astype(jnp.bfloat16)
    joined = jnp.concatenate([conv_cache, active], axis=0)
    rimmed = with_halo(joined, ((ROWS, 1),), 1)
    padded = jnp.pad(rimmed, ((0, 0), (0, 0), (1, 1), (0, 0)))
    summed = conv_bias + jnp.zeros((frame_count * row_count * col_count, channels), jnp.float32)
    for frame_tap in range(3):
        summed = summed + conv_taps(
            padded[frame_tap : frame_tap + frame_count],
            conv_weight[frame_tap],
            row_count,
            col_count,
        )
    block = (signal + summed.reshape(signal.shape)).astype(jnp.bfloat16)
    doubled = temporal(block, time_cache, time_weight, time_bias)
    upsampled = jnp.repeat(jnp.repeat(doubled, 2, axis=1), 2, axis=2)
    upsampled = with_halo(upsampled, ((ROWS, 1),), 1)
    padded_up = jnp.pad(upsampled, ((0, 0), (0, 0), (1, 1), (0, 0)))
    result = conv_taps(padded_up, up_weight, 2 * row_count, 2 * col_count) + up_bias
    return result.astype(jnp.bfloat16).reshape(
        2 * frame_count, 2 * row_count, 2 * col_count, up_weight.shape[-1]
    )


def solution(mesh):
    finer = Mesh(
        mesh.devices.reshape(mesh.shape["parts"], 16, 4, 2), ("parts", "rows_0", "rows_1", "rows_2")
    )
    placed = (
        P("parts", ROWS, None, None),
        P("parts", ROWS, None, None),
        P("parts", ROWS, None, None),
        P(),
        P(),
        P(),
        P(),
        P(),
        P(),
        P(),
        P(),
    )
    return jax.shard_map(
        on_device,
        mesh=finer,
        in_specs=placed,
        out_specs=P("parts", ROWS, None, None),
        check_vma=False,
    )
```

profile of v0, /device:TPU:39, one launch (start us, length us, event | category | flops | bytes accessed | tf_op | source)
XLA Modules:
  0.0 134.7 jit_solution(4475981144398984496)
XLA Ops:
  0.0 1.2 convert_reduce_fusion
  1.6 42.4 %all-reduce.2 = (f32[32]{0:T(128)S(1)}, f32[32]{0:T(128)S(1)}) all-reduce(f32[32]{0:T(128)S(1)} %reduce_sum.37, f32[32]{0:T(128)S(1)} %reduce_sum.25), channel_id=1, replica_groups=mesh['parts'=2,'rows_0'=16,'rows_1'=4,'rows_2'=2] {'rows_0'}, use_global_device_ids=true, to_apply=%region_7.0 | all-reduce | flops 64 | bytes 512 | tf_op jit(solution)/shard_map/psum | solution.py:14
  44.0 5.8 %all-reduce.3 = (f32[32]{0:T(128)S(1)}, f32[32]{0:T(128)S(1)}) all-reduce(f32[32]{0:T(128)S(1)} %get-tuple-element.7, f32[32]{0:T(128)S(1)} %get-tuple-element.8), channel_id=1, replica_groups=mesh['parts'=2,'rows_0'=16,'rows_1'=4,'rows_2'=2] {'rows_1'}, use_global_device_ids=true, to_apply=%region_8.9 | all-reduce | flops 64 | bytes 512 | tf_op jit(solution)/shard_map/psum | solution.py:14
  49.8 11.5 %all-reduce.4 = (f32[32]{0:T(128)S(1)}, f32[32]{0:T(128)S(1)}) all-reduce(f32[32]{0:T(128)S(1)} %get-tuple-element.9, f32[32]{0:T(128)S(1)} %get-tuple-element.10), channel_id=1, replica_groups=mesh['parts'=2,'rows_0'=16,'rows_1'=4,'rows_2'=2] {'rows_2'}, use_global_device_ids=true, to_apply=%region_9.10 | all-reduce | flops 64 | bytes 512 | tf_op jit(solution)/shard_map/psum | solution.py:14
  61.7 1.1 fusion.31
  62.9 1.0 pad_maximum_fusion.13
  63.9 3.8 %collective-permute-start = (bf16[4,1,160,384]{3,2,1,0:T(8,128)(2,1)S(1)}, bf16[4,1,160,384]{3,2,1,0:T(8,128)(2,1)S(1)}, u32[]{:S(2)}, u32[]{:S(2)}) collective-permute-start(bf16[4,1,160,384]{3,2,1,0:T(8,128)(2,1)S(1)} %pad_maximum_fusion.13), channel_id=1, source_target_pairs={{0,1},{1,2},{2,3},{3,4},{4,5},{5,6},{6,7},{7,8},{8,9},{9,10},{10,1... | collective-permute-start | bytes 1474568 | tf_op jit(solution)/shard_map/ppermute | solution.py:25
  67.6 2.0 %collective-permute-start.1 = (bf16[4,1,160,384]{3,2,1,0:T(8,128)(2,1)S(1)}, bf16[4,1,160,384]{3,2,1,0:T(8,128)(2,1)S(1)}, u32[]{:S(2)}, u32[]{:S(2)}) collective-permute-start(bf16[4,1,160,384]{3,2,1,0:T(8,128)(2,1)S(1)} %pad_maximum_fusion.13), channel_id=1, source_target_pairs={{1,0},{2,1},{3,2},{4,3},{5,4},{6,5},{7,6},{8,7},{9,8},{10,9},{11,1... | collective-permute-start | bytes 1474568 | tf_op jit(solution)/shard_map/ppermute | solution.py:26
  69.6 3.9 %fusion.35 = (bf16[1,1,3,384,384]{4,3,2,1,0:T(8,128)(2,1)S(1)}, bf16[1,1,3,384,384]{4,3,2,1,0:T(8,128)(2,1)S(1)}, bf16[1,1,3,384,384]{4,3,2,1,0:T(8,128)(2,1)S(1...) fusion(bf16[3,3,3,384,384]{4,3,2,1,0:T(8,128)(2,1)} %param.16), kind=kLoop, calls=%fused_computation.71 | loop fusion | bytes 15925248 | tf_op jit(solution)/shard_map/slice | solution.py:44
  73.6 6.3 %collective-permute-done.1 = bf16[4,1,160,384]{3,2,1,0:T(8,128)(2,1)S(1)} collective-permute-done((bf16[4,1,160,384]{3,2,1,0:T(8,128)(2,1)S(1)}, bf16[4,1,160,384]{3,2,1,0:T(8,128)(2,1)S(1)}, u32[]{:S(2)}, u32[]{:S(2)}) %collective-permute-start.1) | collective-permute-done | bytes 491552 | tf_op jit(solution)/shard_map/ppermute | solution.py:26
  80.4 0.7 fusion.37
  86.7 0.6 fusion.20
  87.8 0.8 fusion.17
  89.3 1.3 slice.254
  90.6 1.9 %collective-permute-start.2 = (bf16[4,1,320,384]{3,2,0,1:T(8,128)(2,1)}, bf16[4,1,320,384]{3,2,0,1:T(8,128)(2,1)S(1)}, u32[]{:S(2)}, u32[]{:S(2)}) collective-permute-start(bf16[4,1,320,384]{3,2,0,1:T(8,128)(2,1)} %slice.254), channel_id=1, source_target_pairs={{0,1},{1,2},{2,3},{3,4},{4,5},{5,6},{6,7},{7,8},{8,9},{9,10},{10,1... | collective-permute-start | bytes 2949128 | tf_op jit(solution)/shard_map/ppermute | solution.py:25
  92.6 2.6 %collective-permute-start.3 = (bf16[4,1,320,384]{3,2,0,1:T(8,128)(2,1)}, bf16[4,1,320,384]{3,2,0,1:T(8,128)(2,1)S(1)}, u32[]{:S(2)}, u32[]{:S(2)}) collective-permute-start(bf16[4,1,320,384]{3,2,0,1:T(8,128)(2,1)} %slice.254), channel_id=1, source_target_pairs={{1,0},{2,1},{3,2},{4,3},{5,4},{6,5},{7,6},{8,7},{9,8},{10,9},{11,1... | collective-permute-start | bytes 2949128 | tf_op jit(solution)/shard_map/ppermute | solution.py:26
  95.2 1.4 %fusion.38 = (bf16[1,3,384,192]{2,3,1,0:T(8,128)(2,1)S(1)}, bf16[1,3,384,192]{2,3,1,0:T(8,128)(2,1)S(1)}, bf16[1,3,384,192]{2,3,1,0:T(8,128)(2,1)S(1)}) fusion(bf16[3,3,384,192]{2,3,1,0:T(8,128)(2,1)} %param.20), kind=kLoop, calls=%fused_computation.74 | loop fusion | bytes 2654208 | tf_op jit(solution)/shard_map/slice | solution.py:44
  97.0 0.9 copy.29
  98.3 0.9 copy.30
  99.5 0.9 copy.28
  100.4 1.3 broadcast_in_dim.14
  101.7 2.2 %collective-permute-done.2 = bf16[4,1,320,384]{3,2,0,1:T(8,128)(2,1)S(1)} collective-permute-done((bf16[4,1,320,384]{3,2,0,1:T(8,128)(2,1)}, bf16[4,1,320,384]{3,2,0,1:T(8,128)(2,1)S(1)}, u32[]{:S(2)}, u32[]{:S(2)}) %collective-permute-start.2) | collective-permute-done | bytes 983072 | tf_op jit(solution)/shard_map/ppermute | solution.py:25
  103.9 6.4 %collective-permute-done.3 = bf16[4,1,320,384]{3,2,0,1:T(8,128)(2,1)S(1)} collective-permute-done((bf16[4,1,320,384]{3,2,0,1:T(8,128)(2,1)}, bf16[4,1,320,384]{3,2,0,1:T(8,128)(2,1)S(1)}, u32[]{:S(2)}, u32[]{:S(2)}) %collective-permute-start.3) | collective-permute-done | bytes 983072 | tf_op jit(solution)/shard_map/ppermute | solution.py:26
  110.3 1.7 %broadcast_in_dim.15 = bf16[4,2,320,384]{3,2,1,0:T(8,128)(2,1)S(1)} broadcast(bf16[4,320,384]{2,1,0:T(8,128)(2,1)} %broadcast_in_dim.14), dimensions={0,2,3} | broadcast | bytes 2949120 | tf_op jit(solution)/shard_map/broadcast_in_dim | solution.py:109
  112.1 1.3 fusion.9
  113.4 3.5 %fusion.36 = (bf16[4,2,320,384]{3,2,1,0:T(8,128)(2,1)S(1)}, bf16[4,2,320,384]{3,2,1,0:T(8,128)(2,1)S(1)}, bf16[4,2,320,384]{3,2,1,0:T(8,128)(2,1)S(1)}, bf16[4,2...) fusion(bf16[4,4,322,384]{3,2,1,0:T(8,128)(2,1)S(1)} %fusion.9), kind=kLoop, calls=%fused_computation.72 | loop fusion | bytes 23592960 | tf_op jit(solution)/shard_map/slice | solution.py:37
  116.9 5.8 %fusion.4 = (bf16[4,2,320,1152]{3,2,1,0:T(8,128)(2,1)S(1)}, bf16[4,2,320,1152]{3,2,1,0:T(8,128)(2,1)S(1)}, bf16[4,2,320,1152]{3,2,1,0:T(8,128)(2,1)S(1)}) fusion(bf16[4,2,320,384]{3,2,1,0:T(8,128)(2,1)S(1)} %broadcast_in_dim.15, bf16[4,1,320,384]{3,2,1,0:T(8,128)(2,1)} %bitcast.81, bf16[4,2,320,384]{3,2,1,0:T(8,128)(2,1)} %get-tuple-element.26, ...), kind=kLoop, calls=%fused_computation.8 | loop fusion | flops 64880640 | bytes 33423360 | tf_op jit(solution)/shard_map/concatenate | solution.py:35
  122.7 3.2 %fusion.44 = f32[2560,192]{0,1:T(8,128)S(1)} fusion(bf16[2560,1152]{1,0:T(8,128)(2,1)S(1)} %bitcast.79, bf16[1152,192]{0,1:T(8,128)(2,1)} %bitcast.107), kind=kOutput, calls=%fused_computation.80 | convolution fusion | flops 1132462080 | bytes 8306688 | tf_op jit(solution)/shard_map/dot_general | solution.py:42
  125.9 2.1 %fusion.45 = f32[2560,192]{0,1:T(8,128)S(1)} fusion(bf16[2560,1152]{1,0:T(8,128)(2,1)S(1)} %bitcast.78, bf16[1152,192]{0,1:T(8,128)(2,1)S(1)} %bitcast.108), kind=kOutput, calls=%fused_computation.81 | convolution fusion | flops 1132462080 | bytes 8306688 | tf_op jit(solution)/shard_map/dot_general | solution.py:42
  128.1 2.1 %fusion.12 = bf16[2560,192]{0,1:T(8,128)(2,1)S(1)} fusion(f32[2560,192]{0,1:T(8,128)S(1)} %fusion.45, f32[2560,192]{0,1:T(8,128)S(1)} %fusion.44, bf16[2560,1152]{1,0:T(8,128)(2,1)S(1)} %bitcast.77, bf16[1152,192]{0,1:T(8,128)(2,1)S(1)} %bitcast.109, f32[192]{0:T(256)S(1)} %copy-done.9), kind=kOutput, calls=%fused_computation.20 | convolution fusion | flops 1134428160 | bytes 11256576 | tf_op jit(solution)/shard_map/dot_general | solution.py:42
  130.2 2.1 %reshape.144 = bf16[4,2,320,192]{2,1,0,3:T(2,128)(2,1)} reshape(bf16[2560,192]{0,1:T(8,128)(2,1)S(1)} %fusion.12) | data formatting | bytes 1966080 | tf_op jit(solution)/shard_map/reshape | solution.py:113
  132.3 2.4 %copy.27 = bf16[4,2,320,192]{2,3,1,0:T(8,128)(2,1)} copy(bf16[4,2,320,192]{2,1,0,3:T(2,128)(2,1)} %reshape.144) | data formatting | bytes 1966080 | tf_op jit(solution)/shard_map/reshape | solution.py:113
  (59 shorter events, 9.1 us)
Async XLA Ops:
  0.0 87.7 %copy-start = (bf16[3,384,768]{2,1,0:T(8,128)(2,1)S(1)}, bf16[3,384,768]{2,1,0:T(8,128)(2,1)}, u32[]{:S(2)}) copy-start(bf16[3,384,768]{2,1,0:T(8,128)(2,1)} %param.18) | copy-start | bytes 5308420
  0.0 69.6 %copy-start.4 = (bf16[2,1,160,384]{3,2,1,0:T(8,128)(2,1)S(1)}, bf16[2,1,160,384]{3,2,1,0:T(8,128)(2,1)}, u32[]{:S(2)}) copy-start(bf16[2,1,160,384]{3,2,1,0:T(8,128)(2,1)} %param.12) | copy-start | bytes 737284
  63.9 9.7 %collective-permute-start = (bf16[4,1,160,384]{3,2,1,0:T(8,128)(2,1)S(1)}, bf16[4,1,160,384]{3,2,1,0:T(8,128)(2,1)S(1)}, u32[]{:S(2)}, u32[]{:S(2)}) collective-permute-start(bf16[4,1,160,384]{3,2,1,0:T(8,128)(2,1)S(1)} %pad_maximum_fusion.13), channel_id=1, source_target_pairs={{0,1},{1,2},{2,3},{3,4},{4,5},{5,6},{6,7},{7,8},{8,9},{9,10},{10,1... | collective-permute-start | bytes 1474568 | tf_op jit(solution)/shard_map/ppermute | solution.py:25
  67.6 12.3 %collective-permute-start.1 = (bf16[4,1,160,384]{3,2,1,0:T(8,128)(2,1)S(1)}, bf16[4,1,160,384]{3,2,1,0:T(8,128)(2,1)S(1)}, u32[]{:S(2)}, u32[]{:S(2)}) collective-permute-start(bf16[4,1,160,384]{3,2,1,0:T(8,128)(2,1)S(1)} %pad_maximum_fusion.13), channel_id=1, source_target_pairs={{1,0},{2,1},{3,2},{4,3},{5,4},{6,5},{7,6},{8,7},{9,8},{10,9},{11,1... | collective-permute-start | bytes 1474568 | tf_op jit(solution)/shard_map/ppermute | solution.py:26
  84.7 0.7 copy-start.10
  86.6 0.9 copy-start.5
  86.6 1.1 copy-start.8
  86.6 1.1 copy-start.11
  90.6 13.3 %collective-permute-start.2 = (bf16[4,1,320,384]{3,2,0,1:T(8,128)(2,1)}, bf16[4,1,320,384]{3,2,0,1:T(8,128)(2,1)S(1)}, u32[]{:S(2)}, u32[]{:S(2)}) collective-permute-start(bf16[4,1,320,384]{3,2,0,1:T(8,128)(2,1)} %slice.254), channel_id=1, source_target_pairs={{0,1},{1,2},{2,3},{3,4},{4,5},{5,6},{6,7},{7,8},{8,9},{9,10},{10,1... | collective-permute-start | bytes 2949128 | tf_op jit(solution)/shard_map/ppermute | solution.py:25
  92.6 17.8 %collective-permute-start.3 = (bf16[4,1,320,384]{3,2,0,1:T(8,128)(2,1)}, bf16[4,1,320,384]{3,2,0,1:T(8,128)(2,1)S(1)}, u32[]{:S(2)}, u32[]{:S(2)}) collective-permute-start(bf16[4,1,320,384]{3,2,0,1:T(8,128)(2,1)} %slice.254), channel_id=1, source_target_pairs={{1,0},{2,1},{3,2},{4,3},{5,4},{6,5},{7,6},{8,7},{9,8},{10,9},{11,1... | collective-permute-start | bytes 2949128 | tf_op jit(solution)/shard_map/ppermute | solution.py:26
  103.9 8.2 %copy-start.2 = (bf16[4,1,320,384]{3,2,0,1:T(8,128)(2,1)}, bf16[4,1,320,384]{3,2,0,1:T(8,128)(2,1)S(1)}, u32[]{:S(2)}) copy-start(bf16[4,1,320,384]{3,2,0,1:T(8,128)(2,1)S(1)} %collective-permute-done.2) | copy-start | bytes 2949124
  110.3 1.7 %copy-start.3 = (bf16[4,1,320,384]{3,2,0,1:T(8,128)(2,1)}, bf16[4,1,320,384]{3,2,0,1:T(8,128)(2,1)S(1)}, u32[]{:S(2)}) copy-start(bf16[4,1,320,384]{3,2,0,1:T(8,128)(2,1)S(1)} %collective-permute-done.3) | copy-start | bytes 2949124
  122.7 3.2 %copy-start.6 = (bf16[24,8,3,384]{3,1,2,0:T(8,128)(2,1)S(1)}, bf16[24,8,3,384]{3,1,2,0:T(8,128)(2,1)}, u32[]{:S(2)}) copy-start(bf16[24,8,3,384]{3,1,2,0:T(8,128)(2,1)} %copy.30) | copy-start | bytes 1327108
  125.9 2.1 %copy-start.7 = (bf16[24,8,3,384]{3,1,2,0:T(8,128)(2,1)S(1)}, bf16[24,8,3,384]{3,1,2,0:T(8,128)(2,1)}, u32[]{:S(2)}) copy-start(bf16[24,8,3,384]{3,1,2,0:T(8,128)(2,1)} %copy.28) | copy-start | bytes 1327108
  125.9 2.1 %copy-start.9 = (f32[192]{0:T(256)S(1)}, f32[192]{0:T(256)}, u32[]{:S(2)}) copy-start(f32[192]{0:T(256)} %param.21) | copy-start | bytes 2308
  128.1 6.6 %copy-start.1 = (bf16[3,384,768]{2,1,0:T(8,128)(2,1)S(1)}, bf16[3,384,768]{2,1,0:T(8,128)(2,1)}, u32[]{:S(2)}) copy-start(bf16[3,384,768]{2,1,0:T(8,128)(2,1)} %param.18) | copy-start | bytes 5308420
where the time goes:
time: 135 us
  blocking collectives  59.7 us (44%)
  local copies, waits for them, and re-layouts  24 us (18%)
  waiting for transfers between devices  14.9 us (11%)
  matrix products  13.5 us (10%)
  other arithmetic  11.9 us (9%)
  starting transfers between devices  10.3 us (8%)
    psum x3, blocking collectives, over_axes(): value = lax.psum(value, axis)  59.7 us
    ppermute x2, waiting for transfers between devices, with_halo(): after = lax.ppermute(initial, axis, down)  12.7 us
    dot_general x12, matrix products, conv_taps(): jnp.dot(window.reshape(-1, 3 * channels), kernel[row_tap].reshape(3 * cha...  12.7 us
    slice x5, local copies, waits for them, and re-layouts, conv_taps(): kernel[row_tap].reshape(3 * channels, -1)  6.51 us
    concatenate x6, other arithmetic, conv_taps(): jnp.concatenate([padded[:, row_tap:row_tap + row_count, col_tap:col_tap +...  6.42 us
    ppermute x2, starting transfers between devices, with_halo(): before = lax.ppermute(last, axis, up)  5.69 us
    ppermute x2, starting transfers between devices, with_halo(): after = lax.ppermute(initial, axis, down)  4.57 us
    reshape x2, local copies, waits for them, and re-layouts, on_device(): result.astype(jnp.bfloat16)  4.54 us
  transfers between devices with their start and end apart: 4, of which 3 were waited for; matrix products, arithmetic and copies ran while one was open for 8% of the time, Pallas kernels for 0%

commit v1 on v0

--- a/solution.py
+++ b/solution.py
@@ -11,7 +11,7 @@
 
 def over_axes(value, axes):
     for axis in axes:
-        value = lax.psum(value, axis)
+        value = jnp.sum(lax.all_gather(value, axis), 0)
     return value
 
 

time: 135 us -> 143 us (1.059)
  local copies, waits for them, and re-layouts: 24 us -> 29.5 us
  between operations: 0.44 us -> 2.42 us
    psum x3 -> x0, blocking collectives: 59.7 us -> none  [over_axes(): value = lax.psum(value, axis)]
    unnamed x0 -> x3, blocking collectives: none -> 59.6 us
    unnamed x27 -> x42, local copies, waits for them, and re-layouts: 3.04 us -> 8.12 us
  transfers between devices with their start and end apart: 4 -> 4, of which waited for: 3 -> 3; matrix products, arithmetic and copies ran while one was open for 8% -> 7% of each run, Pallas kernels for 0% -> 0%
where the time goes in v1:
time: 143 us; the launch traced here: 142 us
  blocking collectives  59.6 us (42%)
  local copies, waits for them, and re-layouts  29.5 us (21%)
  waiting for transfers between devices  15 us (10%)
  matrix products  13.5 us (9%)
  other arithmetic  12 us (8%)
  starting transfers between devices  10.2 us (7%)
  between operations  2.42 us (2%)
    unnamed x3, blocking collectives  59.6 us
    ppermute x2, waiting for transfers between devices, with_halo(): after = lax.ppermute(initial, axis, down)  12.7 us
    dot_general x12, matrix products, conv_taps(): jnp.dot(window.reshape(-1, 3 * channels), kernel[row_tap].reshape(3 * cha...  12.7 us
    unnamed x42, local copies, waits for them, and re-layouts  8.12 us
    slice x5, local copies, waits for them, and re-layouts, conv_taps(): kernel[row_tap].reshape(3 * channels, -1)  6.51 us
    concatenate x6, other arithmetic, conv_taps(): jnp.concatenate([padded[:, row_tap:row_tap + row_count, col_tap:col_tap +...  6.42 us
    ppermute x2, starting transfers between devices, with_halo(): before = lax.ppermute(last, axis, up)  5.68 us
    ppermute x2, starting transfers between devices, with_halo(): after = lax.ppermute(initial, axis, down)  4.57 us
  transfers between devices with their start and end apart: 4, of which 3 were waited for; matrix products, arithmetic and copies ran while one was open for 7% of the time, Pallas kernels for 0%

profile of v1, /device:TPU:39, one launch (start us, length us, event | category | flops | bytes accessed | tf_op | source)
XLA Modules:
  0.0 142.4 jit_solution(709173864324018622)
XLA Ops:
  0.0 1.2 convert_reduce_fusion
  1.4 1.3 dynamic-slice
  4.0 42.4 %all-reduce.8 = (f32[512]{0:T(512)S(1)}, f32[512]{0:T(512)S(1)}) all-reduce(f32[512]{0:T(512)S(1)} %dynamic-update-slice.3, f32[512]{0:T(512)S(1)} %dynamic-update-slice), channel_id=5, replica_groups=mesh['parts'=2,'rows_0'=16,'rows_1'=4,'rows_2'=2] {'rows_0'}, use_global_device_ids=true, to_apply=%add.5 | all-reduce | flops 1024 | bytes 8192
  46.5 1.3 dynamic-slice.1
  48.9 5.8 %all-reduce.9 = (f32[128]{0:T(128)S(1)}, f32[128]{0:T(128)S(1)}) all-reduce(f32[128]{0:T(128)S(1)} %dynamic-update-slice.4, f32[128]{0:T(128)S(1)} %dynamic-update-slice.1), channel_id=6, replica_groups=mesh['parts'=2,'rows_0'=16,'rows_1'=4,'rows_2'=2] {'rows_1'}, use_global_device_ids=true, to_apply=%add.6 | all-reduce | flops 256 | bytes 2048
  54.8 1.3 dynamic-slice.2
  57.3 11.5 %all-reduce.10 = (f32[64]{0:T(128)S(1)}, f32[64]{0:T(128)S(1)}) all-reduce(f32[64]{0:T(128)S(1)} %dynamic-update-slice.5, f32[64]{0:T(128)S(1)} %dynamic-update-slice.2), channel_id=7, replica_groups=mesh['parts'=2,'rows_0'=16,'rows_1'=4,'rows_2'=2] {'rows_2'}, use_global_device_ids=true, to_apply=%add.7 | all-reduce | flops 128 | bytes 1024
  69.4 1.1 fusion.31
  70.5 1.0 pad_maximum_fusion.13
  71.5 3.7 %collective-permute-start = (bf16[4,1,160,384]{3,2,1,0:T(8,128)(2,1)S(1)}, bf16[4,1,160,384]{3,2,1,0:T(8,128)(2,1)S(1)}, u32[]{:S(2)}, u32[]{:S(2)}) collective-permute-start(bf16[4,1,160,384]{3,2,1,0:T(8,128)(2,1)S(1)} %pad_maximum_fusion.13), channel_id=1, source_target_pairs={{0,1},{1,2},{2,3},{3,4},{4,5},{5,6},{6,7},{7,8},{8,9},{9,10},{10,1... | collective-permute-start | bytes 1474568 | tf_op jit(solution)/shard_map/ppermute | solution.py:25
  75.3 2.0 %collective-permute-start.1 = (bf16[4,1,160,384]{3,2,1,0:T(8,128)(2,1)S(1)}, bf16[4,1,160,384]{3,2,1,0:T(8,128)(2,1)S(1)}, u32[]{:S(2)}, u32[]{:S(2)}) collective-permute-start(bf16[4,1,160,384]{3,2,1,0:T(8,128)(2,1)S(1)} %pad_maximum_fusion.13), channel_id=1, source_target_pairs={{1,0},{2,1},{3,2},{4,3},{5,4},{6,5},{7,6},{8,7},{9,8},{10,9},{11,1... | collective-permute-start | bytes 1474568 | tf_op jit(solution)/shard_map/ppermute | solution.py:26
  77.3 3.9 %fusion.35 = (bf16[1,1,3,384,384]{4,3,2,1,0:T(8,128)(2,1)S(1)}, bf16[1,1,3,384,384]{4,3,2,1,0:T(8,128)(2,1)S(1)}, bf16[1,1,3,384,384]{4,3,2,1,0:T(8,128)(2,1)S(1...) fusion(bf16[3,3,3,384,384]{4,3,2,1,0:T(8,128)(2,1)} %param.16), kind=kLoop, calls=%fused_computation.71 | loop fusion | bytes 15925248 | tf_op jit(solution)/shard_map/slice | solution.py:44
  81.3 6.3 %collective-permute-done.1 = bf16[4,1,160,384]{3,2,1,0:T(8,128)(2,1)S(1)} collective-permute-done((bf16[4,1,160,384]{3,2,1,0:T(8,128)(2,1)S(1)}, bf16[4,1,160,384]{3,2,1,0:T(8,128)(2,1)S(1)}, u32[]{:S(2)}, u32[]{:S(2)}) %collective-permute-start.1) | collective-permute-done | bytes 491552 | tf_op jit(solution)/shard_map/ppermute | solution.py:26
  97.0 1.3 slice.254
  98.3 1.9 %collective-permute-start.2 = (bf16[4,1,320,384]{3,2,0,1:T(8,128)(2,1)}, bf16[4,1,320,384]{3,2,0,1:T(8,128)(2,1)S(1)}, u32[]{:S(2)}, u32[]{:S(2)}) collective-permute-start(bf16[4,1,320,384]{3,2,0,1:T(8,128)(2,1)} %slice.254), channel_id=1, source_target_pairs={{0,1},{1,2},{2,3},{3,4},{4,5},{5,6},{6,7},{7,8},{8,9},{9,10},{10,1... | collective-permute-start | bytes 2949128 | tf_op jit(solution)/shard_map/ppermute | solution.py:25
  100.2 2.6 %collective-permute-start.3 = (bf16[4,1,320,384]{3,2,0,1:T(8,128)(2,1)}, bf16[4,1,320,384]{3,2,0,1:T(8,128)(2,1)S(1)}, u32[]{:S(2)}, u32[]{:S(2)}) collective-permute-start(bf16[4,1,320,384]{3,2,0,1:T(8,128)(2,1)} %slice.254), channel_id=1, source_target_pairs={{1,0},{2,1},{3,2},{4,3},{5,4},{6,5},{7,6},{8,7},{9,8},{10,9},{11,1... | collective-permute-start | bytes 2949128 | tf_op jit(solution)/shard_map/ppermute | solution.py:26
  102.8 1.4 fusion.38
  104.7 0.9 copy.39
  105.9 0.8 copy.40
  107.1 0.9 copy.38
  108.0 1.3 broadcast_in_dim.14
  109.3 2.3 %collective-permute-done.2 = bf16[4,1,320,384]{3,2,0,1:T(8,128)(2,1)S(1)} collective-permute-done((bf16[4,1,320,384]{3,2,0,1:T(8,128)(2,1)}, bf16[4,1,320,384]{3,2,0,1:T(8,128)(2,1)S(1)}, u32[]{:S(2)}, u32[]{:S(2)}) %collective-permute-start.2) | collective-permute-done | bytes 983072 | tf_op jit(solution)/shard_map/ppermute | solution.py:25
  111.6 6.4 %collective-permute-done.3 = bf16[4,1,320,384]{3,2,0,1:T(8,128)(2,1)S(1)} collective-permute-done((bf16[4,1,320,384]{3,2,0,1:T(8,128)(2,1)}, bf16[4,1,320,384]{3,2,0,1:T(8,128)(2,1)S(1)}, u32[]{:S(2)}, u32[]{:S(2)}) %collective-permute-start.3) | collective-permute-done | bytes 983072 | tf_op jit(solution)/shard_map/ppermute | solution.py:26
  118.0 1.7 %broadcast_in_dim.15 = bf16[4,2,320,384]{3,2,1,0:T(8,128)(2,1)S(1)} broadcast(bf16[4,320,384]{2,1,0:T(8,128)(2,1)} %broadcast_in_dim.14), dimensions={0,2,3} | broadcast | bytes 2949120 | tf_op jit(solution)/shard_map/broadcast_in_dim | solution.py:109
  119.7 1.3 fusion.9
  121.1 3.5 %fusion.36 = (bf16[4,2,320,384]{3,2,1,0:T(8,128)(2,1)S(1)}, bf16[4,2,320,384]{3,2,1,0:T(8,128)(2,1)S(1)}, bf16[4,2,320,384]{3,2,1,0:T(8,128)(2,1)S(1)}, bf16[4,2...) fusion(bf16[4,4,322,384]{3,2,1,0:T(8,128)(2,1)S(1)} %fusion.9), kind=kLoop, calls=%fused_computation.72 | loop fusion | bytes 23592960 | tf_op jit(solution)/shard_map/slice | solution.py:37
  124.5 5.8 %fusion.4 = (bf16[4,2,320,1152]{3,2,1,0:T(8,128)(2,1)S(1)}, bf16[4,2,320,1152]{3,2,1,0:T(8,128)(2,1)S(1)}, bf16[4,2,320,1152]{3,2,1,0:T(8,128)(2,1)S(1)}) fusion(bf16[4,2,320,384]{3,2,1,0:T(8,128)(2,1)S(1)} %broadcast_in_dim.15, bf16[4,1,320,384]{3,2,1,0:T(8,128)(2,1)} %bitcast.84, bf16[4,2,320,384]{3,2,1,0:T(8,128)(2,1)} %get-tuple-element.26, ...), kind=kLoop, calls=%fused_computation.8 | loop fusion | flops 64880640 | bytes 33423360 | tf_op jit(solution)/shard_map/concatenate | solution.py:35
  130.4 3.2 %fusion.44 = f32[2560,192]{0,1:T(8,128)S(1)} fusion(bf16[2560,1152]{1,0:T(8,128)(2,1)S(1)} %bitcast.82, bf16[1152,192]{0,1:T(8,128)(2,1)} %bitcast.110), kind=kOutput, calls=%fused_computation.80 | convolution fusion | flops 1132462080 | bytes 8306688 | tf_op jit(solution)/shard_map/dot_general | solution.py:42
  133.6 2.1 %fusion.45 = f32[2560,192]{0,1:T(8,128)S(1)} fusion(bf16[2560,1152]{1,0:T(8,128)(2,1)S(1)} %bitcast.81, bf16[1152,192]{0,1:T(8,128)(2,1)S(1)} %bitcast.111), kind=kOutput, calls=%fused_computation.81 | convolution fusion | flops 1132462080 | bytes 8306688 | tf_op jit(solution)/shard_map/dot_general | solution.py:42
  135.7 2.1 %fusion.12 = bf16[2560,192]{0,1:T(8,128)(2,1)S(1)} fusion(f32[2560,192]{0,1:T(8,128)S(1)} %fusion.45, f32[2560,192]{0,1:T(8,128)S(1)} %fusion.44, bf16[2560,1152]{1,0:T(8,128)(2,1)S(1)} %bitcast.80, bf16[1152,192]{0,1:T(8,128)(2,1)S(1)} %bitcast.112, f32[192]{0:T(256)S(1)} %copy-done.9), kind=kOutput, calls=%fused_computation.20 | convolution fusion | flops 1134428160 | bytes 11256576 | tf_op jit(solution)/shard_map/dot_general | solution.py:42
  137.8 2.1 %reshape.154 = bf16[4,2,320,192]{2,1,0,3:T(2,128)(2,1)} reshape(bf16[2560,192]{0,1:T(8,128)(2,1)S(1)} %fusion.12) | data formatting | bytes 1966080 | tf_op jit(solution)/shard_map/reshape | solution.py:113
  139.9 2.4 %copy.37 = bf16[4,2,320,192]{2,3,1,0:T(8,128)(2,1)} copy(bf16[4,2,320,192]{2,1,0,3:T(2,128)(2,1)} %reshape.154) | data formatting | bytes 1966080 | tf_op jit(solution)/shard_map/reshape | solution.py:113
  (86 shorter events, 13.1 us)
Async XLA Ops:
  0.0 95.4 %copy-start = (bf16[3,384,768]{2,1,0:T(8,128)(2,1)S(1)}, bf16[3,384,768]{2,1,0:T(8,128)(2,1)}, u32[]{:S(2)}) copy-start(bf16[3,384,768]{2,1,0:T(8,128)(2,1)} %param.18) | copy-start | bytes 5308420
  0.0 77.2 %copy-start.4 = (bf16[2,1,160,384]{3,2,1,0:T(8,128)(2,1)S(1)}, bf16[2,1,160,384]{3,2,1,0:T(8,128)(2,1)}, u32[]{:S(2)}) copy-start(bf16[2,1,160,384]{3,2,1,0:T(8,128)(2,1)} %param.12) | copy-start | bytes 737284
  71.5 9.7 %collective-permute-start = (bf16[4,1,160,384]{3,2,1,0:T(8,128)(2,1)S(1)}, bf16[4,1,160,384]{3,2,1,0:T(8,128)(2,1)S(1)}, u32[]{:S(2)}, u32[]{:S(2)}) collective-permute-start(bf16[4,1,160,384]{3,2,1,0:T(8,128)(2,1)S(1)} %pad_maximum_fusion.13), channel_id=1, source_target_pairs={{0,1},{1,2},{2,3},{3,4},{4,5},{5,6},{6,7},{7,8},{8,9},{9,10},{10,1... | collective-permute-start | bytes 1474568 | tf_op jit(solution)/shard_map/ppermute | solution.py:25
  75.3 12.3 %collective-permute-start.1 = (bf16[4,1,160,384]{3,2,1,0:T(8,128)(2,1)S(1)}, bf16[4,1,160,384]{3,2,1,0:T(8,128)(2,1)S(1)}, u32[]{:S(2)}, u32[]{:S(2)}) collective-permute-start(bf16[4,1,160,384]{3,2,1,0:T(8,128)(2,1)S(1)} %pad_maximum_fusion.13), channel_id=1, source_target_pairs={{1,0},{2,1},{3,2},{4,3},{5,4},{6,5},{7,6},{8,7},{9,8},{10,9},{11,1... | collective-permute-start | bytes 1474568 | tf_op jit(solution)/shard_map/ppermute | solution.py:26
  92.4 0.7 copy-start.10
  94.3 0.9 copy-start.5
  94.3 1.1 copy-start.8
  94.3 1.1 copy-start.11
  98.3 13.3 %collective-permute-start.2 = (bf16[4,1,320,384]{3,2,0,1:T(8,128)(2,1)}, bf16[4,1,320,384]{3,2,0,1:T(8,128)(2,1)S(1)}, u32[]{:S(2)}, u32[]{:S(2)}) collective-permute-start(bf16[4,1,320,384]{3,2,0,1:T(8,128)(2,1)} %slice.254), channel_id=1, source_target_pairs={{0,1},{1,2},{2,3},{3,4},{4,5},{5,6},{6,7},{7,8},{8,9},{9,10},{10,1... | collective-permute-start | bytes 2949128 | tf_op jit(solution)/shard_map/ppermute | solution.py:25
  100.2 17.8 %collective-permute-start.3 = (bf16[4,1,320,384]{3,2,0,1:T(8,128)(2,1)}, bf16[4,1,320,384]{3,2,0,1:T(8,128)(2,1)S(1)}, u32[]{:S(2)}, u32[]{:S(2)}) collective-permute-start(bf16[4,1,320,384]{3,2,0,1:T(8,128)(2,1)} %slice.254), channel_id=1, source_target_pairs={{1,0},{2,1},{3,2},{4,3},{5,4},{6,5},{7,6},{8,7},{9,8},{10,9},{11,1... | collective-permute-start | bytes 2949128 | tf_op jit(solution)/shard_map/ppermute | solution.py:26
  111.6 8.2 %copy-start.2 = (bf16[4,1,320,384]{3,2,0,1:T(8,128)(2,1)}, bf16[4,1,320,384]{3,2,0,1:T(8,128)(2,1)S(1)}, u32[]{:S(2)}) copy-start(bf16[4,1,320,384]{3,2,0,1:T(8,128)(2,1)S(1)} %collective-permute-done.2) | copy-start | bytes 2949124
  118.0 1.7 %copy-start.3 = (bf16[4,1,320,384]{3,2,0,1:T(8,128)(2,1)}, bf16[4,1,320,384]{3,2,0,1:T(8,128)(2,1)S(1)}, u32[]{:S(2)}) copy-start(bf16[4,1,320,384]{3,2,0,1:T(8,128)(2,1)S(1)} %collective-permute-done.3) | copy-start | bytes 2949124
  130.4 3.2 %copy-start.6 = (bf16[24,8,3,384]{3,1,2,0:T(8,128)(2,1)S(1)}, bf16[24,8,3,384]{3,1,2,0:T(8,128)(2,1)}, u32[]{:S(2)}) copy-start(bf16[24,8,3,384]{3,1,2,0:T(8,128)(2,1)} %copy.40) | copy-start | bytes 1327108
  133.6 2.1 %copy-start.7 = (bf16[24,8,3,384]{3,1,2,0:T(8,128)(2,1)S(1)}, bf16[24,8,3,384]{3,1,2,0:T(8,128)(2,1)}, u32[]{:S(2)}) copy-start(bf16[24,8,3,384]{3,1,2,0:T(8,128)(2,1)} %copy.38) | copy-start | bytes 1327108
  133.6 2.1 %copy-start.9 = (f32[192]{0:T(256)S(1)}, f32[192]{0:T(256)}, u32[]{:S(2)}) copy-start(f32[192]{0:T(256)} %param.21) | copy-start | bytes 2308
  135.7 6.6 %copy-start.1 = (bf16[3,384,768]{2,1,0:T(8,128)(2,1)S(1)}, bf16[3,384,768]{2,1,0:T(8,128)(2,1)}, u32[]{:S(2)}) copy-start(bf16[3,384,768]{2,1,0:T(8,128)(2,1)} %param.18) | copy-start | bytes 5308420
